TPU v7x, 256 devices: a whole 4x4x8 slice. The times are simulated.
256 devices in a mesh: grid: 2 (over core), px: 16 (over y, x), py: 8 (over z).
Axes of the slice: x: 4, y: 4, z: 8, core: 2. Of those that a mesh axis runs over, the one named last changes fastest.
Arguments:
- residual: float32 [2, 128, 64, 5, 1024], P('grid', 'px', 'py'), may hold values from -3 to 3
- inverses: float32 [2, 128, 64, 25, 1024], P('grid', 'px', 'py'), may hold values from 0 to 1, as said below
- couplings: float32 [2, 128, 64, 4, 1024], P('grid', 'px', 'py'), may hold values from 0.22 to 0.735, as said below
- receptors: int32 [2, 16, 8, 512], P('grid', 'px', 'py'), may hold values from 0 to 65535, as said below
- owners: int32 [2, 16, 8, 512, 1], P('grid', 'px', 'py'), may hold values from 0 to 127; in each aligned block of 512 rows (0 to 511, 512 to 1023, ..., all dimensions but the last counted through in order) at most 8 rows name the same one
- donors: int32 [2, 16, 8, 512, 8], P('grid', 'px', 'py'), may hold values from 0 to 65535
- weights: float32 [2, 16, 8, 512, 8], P('grid', 'px', 'py'), may hold values from 0 to 1, as said below
Outputs:
- update: float32 [2, 128, 64, 5, 1024], P('grid', 'px', 'py')
Inputs may be any that keep to these rules, and one draw needn't show every extreme that they name: `receptors`: receptor indices of one device are distinct. `owners`: among the receptors of one device no owner appears more than 8 times, and in every draw some device names one owner exactly 8 times. `weights`: nonnegative; the 8 weights of a receptor sum to 1. `inverses`: all entries nonnegative; off-diagonal entries 0.02 to 0.07; each row of a block sums to 0.94 to 1. `couplings`: a + b and e + f of each cell lie in 0.88 to 0.98, and each coupling is a quarter to three quarters of its pair's sum.
All inputs are finite; a program needn't handle non-finite values.
Results may differ from a plain program's by a relative error of at most 0.0001.
Values sent between devices are 32-bit elements; how exact they have to be, the bound alone decides.
A program may use at most 128 MiB of HBM per device.

v0:
```python
import jax
import jax.numpy as jnp
from jax import lax
from jax.sharding import PartitionSpec as P

KBLOCKS = 8


def from_behind(block, axis, distance):
    devices = range(lax.axis_size(axis))
    route = [(i - distance, i) for i in devices if i - distance in devices]
    return lax.ppermute(block, axis, route)


def swapped(array, axis, distance):
    return lax.ppermute(array, axis, [(i, i ^ 1 << distance) for i in range(lax.axis_size(axis))])


def grouped_exchange(array, axis, split_dim, concat_dim, work, item_dim, out_dim):
    items = jax.tree.leaves(array)[0].shape[item_dim]
    count = 2 if items % 2 == 0 else 1
    gathered = []
    for k in range(count):
        group = jax.tree.map(
            lambda a: lax.slice_in_dim(
                a, k * (items // count), (k + 1) * (items // count), axis=item_dim
            ),
            array,
        )
        gathered.append(
            work(
                lax.all_to_all(
                    group, axis, split_axis=split_dim, concat_axis=concat_dim, tiled=True
                )
            )
        )
    return jax.tree.map(lambda *parts: jnp.concatenate(parts, axis=out_dim), *gathered)


def apply_block(block, vector):
    shaped = block.reshape(block.shape[:-2] + (5, 5, block.shape[-1]))
    return jnp.sum(shaped * vector[..., None, :, :], axis=-2)


def sweep_forward(rhs_part, inverse_part, coupling_part, from_rows, from_columns):

    def row_step(upper_row, inputs):
        rhs_row, inv_row, coup_row, left_start = inputs
        left_value = left_start
        cell_list = []
        for column in range(rhs_row.shape[0]):
            left_value = apply_block(
                inv_row[column],
                rhs_row[column]
                + coup_row[column, 0][None] * upper_row[column]
                + coup_row[column, 1][None] * left_value,
            )
            cell_list.append(left_value)
        row_values = jnp.stack(cell_list)
        return (row_values, row_values)

    _, result = lax.scan(row_step, from_rows, (rhs_part, inverse_part, coupling_part, from_columns))
    return result


def sweep_backward(star_part, inverse_part, coupling_part, from_rows, from_columns):

    def row_step(lower_row, inputs):
        star_row, inv_row, coup_row, right_start = inputs
        right_value = right_start
        cell_list = [None] * star_row.shape[0]
        for column in reversed(range(star_row.shape[0])):
            right_value = star_row[column] + apply_block(
                inv_row[column],
                coup_row[column, 2][None] * lower_row[column]
                + coup_row[column, 3][None] * right_value,
            )
            cell_list[column] = right_value
        row_values = jnp.stack(cell_list)
        return (row_values, row_values)

    _, result = lax.scan(
        row_step, from_rows, (star_part, inverse_part, coupling_part, from_columns), reverse=True
    )
    return result


def local(residual, inverses, couplings, receptors, owners, donors, weights):
    rhs_local = residual[0]
    inverse_local = inverses[0]
    coupling_local = couplings[0]
    row_count, col_count, comp_count, pencil_length = rhs_local.shape
    block_count = KBLOCKS
    block_width = pencil_length // block_count
    place_rows = lax.axis_index("px")
    place_cols = lax.axis_index("py")
    count_rows = lax.axis_size("px")
    count_cols = lax.axis_size("py")
    sections = count_rows + count_cols - 1 + block_count - 1
    face_rows = jnp.zeros((col_count, comp_count, block_width), jnp.float32)
    face_cols = jnp.zeros((row_count, comp_count, block_width), jnp.float32)

    def slices(offset):
        return (
            lax.dynamic_slice_in_dim(inverse_local, offset, block_width, 3),
            lax.dynamic_slice_in_dim(coupling_local, offset, block_width, 3),
        )

    def forward_section(section_number, state_now):
        field_now, rows_now, cols_now = state_now
        from_rows = from_behind(rows_now, "px", 1)
        from_columns = from_behind(cols_now, "py", 1)
        block_index = section_number - place_rows - place_cols
        active = (block_index >= 0) & (block_index < block_count)
        offset = jnp.clip(block_index, 0, block_count - 1) * block_width

        def forward_compute(unused):
            inverse_part, coupling_part = slices(offset)
            rhs_part = lax.dynamic_slice_in_dim(rhs_local, offset, block_width, 3)
            result = sweep_forward(rhs_part, inverse_part, coupling_part, from_rows, from_columns)
            return (
                lax.dynamic_update_slice_in_dim(field_now, result, offset, 3),
                result[-1],
                result[:, -1],
            )

        def forward_keep(unused):
            return (field_now, rows_now, cols_now)

        return lax.cond(active, forward_compute, forward_keep, None)

    star_field = jnp.zeros_like(rhs_local)
    star_field, _, _ = lax.fori_loop(
        0, sections, forward_section, (star_field, face_rows, face_cols)
    )

    def backward_section(section_number, state_now):
        field_now, rows_now, cols_now = state_now
        from_rows = from_behind(rows_now, "px", -1)
        from_columns = from_behind(cols_now, "py", -1)
        block_index = section_number - (count_rows - 1 - place_rows) - (count_cols - 1 - place_cols)
        active = (block_index >= 0) & (block_index < block_count)
        offset = jnp.clip(block_index, 0, block_count - 1) * block_width

        def backward_compute(unused):
            inverse_part, coupling_part = slices(offset)
            star_part = lax.dynamic_slice_in_dim(star_field, offset, block_width, 3)
            result = sweep_backward(star_part, inverse_part, coupling_part, from_rows, from_columns)
            return (
                lax.dynamic_update_slice_in_dim(field_now, result, offset, 3),
                result[0],
                result[:, 0],
            )

        def backward_keep(unused):
            return (field_now, rows_now, cols_now)

        return lax.cond(active, backward_compute, backward_keep, None)

    swept_field = jnp.zeros_like(rhs_local)
    swept_field, _, _ = lax.fori_loop(
        0, sections, backward_section, (swept_field, face_rows, face_cols)
    )
    receptor_list = receptors[0, 0, 0]
    owner_list = owners[0, 0, 0, :, 0]
    donor_list = donors[0, 0, 0]
    weight_list = weights[0, 0, 0]
    receptor_count = receptor_list.shape[0]
    owner_count = count_rows * count_cols
    slot_count = max(2, 2 * receptor_count // owner_count)
    onehot = (owner_list[:, None] == jnp.arange(owner_count, dtype=jnp.int32)[None, :]).astype(
        jnp.int32
    )
    slot_rank = jnp.sum((jnp.cumsum(onehot, axis=0) - 1) * onehot, axis=1)
    slot_place = owner_list * slot_count + slot_rank
    request = (
        jnp.zeros((owner_count * slot_count, donor_list.shape[1]), jnp.int32)
        .at[slot_place]
        .set(donor_list)
    )
    request = request.reshape(owner_count, slot_count, donor_list.shape[1])
    flat_cells = swept_field.reshape(row_count * col_count, comp_count, pencil_length)

    def lookup(index_list):
        return flat_cells[index_list // pencil_length, :, index_list % pencil_length]

    moved_index = swapped(request, "grid", 0)
    values = grouped_exchange(moved_index, ("px", "py"), 0, 0, lookup, 1, 1)
    returned = lax.all_to_all(values, ("px", "py"), split_axis=0, concat_axis=0, tiled=True)
    returned = swapped(returned, "grid", 0)
    gathered = returned.reshape(owner_count * slot_count, donor_list.shape[1], comp_count)[
        slot_place
    ]
    fringe_values = jnp.sum(gathered * weight_list[..., None], axis=-2)
    refreshed = flat_cells.at[receptor_list // pencil_length, :, receptor_list % pencil_length].set(
        fringe_values
    )
    return refreshed.reshape(row_count, col_count, comp_count, pencil_length)[None]


def solution(mesh):
    placed = (
        P("grid", "px", "py", None, None),
        P("grid", "px", "py", None, None),
        P("grid", "px", "py", None, None),
        P("grid", "px", "py", None),
        P("grid", "px", "py", None, None),
        P("grid", "px", "py", None, None),
        P("grid", "px", "py", None, None),
    )
    return jax.shard_map(
        local,
        mesh=mesh,
        in_specs=placed,
        out_specs=P("grid", "px", "py", None, None),
        check_vma=False,
    )
```

profile of v0, /device:TPU:1, one launch (start us, length us, event | category | flops | bytes accessed | tf_op | source)
XLA Modules:
  0.0 1433.8 jit_solution(4124557084871150595)
XLA Ops:
  11.0 10.3 copy.93
  22.2 13.8 all-to-all-start
  37.6 380.9 %while.69 = (s32[]{:T(128)}, f32[8,8,5,1024]{3,2,1,0:T(8,128)}, f32[8,5,128]{2,1,0:T(8,128)S(1)}, f32[8,5,128]{2,1,0:T(8,128)S(1)}, s32[]{:T(128)}, /*index=5*/s...) while((s32[]{:T(128)}, f32[8,8,5,1024]{3,2,1,0:T(8,128)}, ...), condition=%wide.region_13.14_spmd, body=%wide.region_0.13_spmd.sunk | while | flops 66582 | bytes 3787170 | solution.py:133
  160.6 10.5 collective-permute-start.2
  177.7 12.2 collective-permute-start.3
  217.9 10.3 collective-permute-start.3
  231.2 9.8 collective-permute-start.3
  244.4 9.9 collective-permute-start.3
  257.2 10.2 collective-permute-start.3
  270.4 9.8 collective-permute-start.3
  296.4 11.5 collective-permute-start.3
  420.0 539.2 %while.70 = (s32[]{:T(128)}, f32[8,8,5,1024]{3,2,1,0:T(8,128)}, f32[8,5,128]{2,1,0:T(8,128)S(1)}, f32[8,5,128]{2,1,0:T(8,128)S(1)}, s32[]{:T(128)}, /*index=5*/s...) while((s32[]{:T(128)}, f32[8,8,5,1024]{3,2,1,0:T(8,128)}, ...), condition=%wide.region_27.28_spmd, body=%wide.region_14.27_spmd.sunk | while | flops 71063 | bytes 3927542 | solution.py:161
  624.0 195.6 %collective-permute-done = f32[8,5,128]{2,1,0:T(8,128)S(1)} collective-permute-done((f32[8,5,128]{2,1,0:T(8,128)S(1)}, f32[8,5,128]{2,1,0:T(8,128)S(1)}, u32[]{:S(2)}, u32[]{:S(2)}) %collective-permute-start) | collective-permute-done | bytes 20512 | tf_op jit(solution)/shard_map/while/body/eval_jaxpr/ppermute | solution.py:12
  819.6 9.7 conditional.5
  838.1 9.8 conditional.5
  912.7 9.7 conditional.5
  959.3 18.0 %copy.74 = f32[8,8,5,1024]{2,3,1,0:T(8,128)} copy(f32[8,8,5,1024]{3,2,1,0:T(8,128)} %get-tuple-element.674) | data formatting | bytes 2621440 | tf_op jit(solution)/shard_map/while | solution.py:161
  984.6 11.6 all-to-all-done.1
  997.1 172.6 %gather_fusion.1 = f32[4096,5]{1,0:T(8,128)S(1)} fusion(f32[64,5,1024]{1,2,0:T(8,128)} %bitcast.503, s32[4096]{0:T(1024)S(1)} %reshape.1313), kind=kCustom, calls=%fused_computation.1 | custom fusion | bytes 196608 | tf_op jit(solution)/shard_map/gather | solution.py:185
  1174.0 60.7 %gather_fusion = f32[4096,5]{1,0:T(8,128)S(1)} fusion(f32[64,5,1024]{1,2,0:T(8,128)} %bitcast.504, s32[4096]{0:T(1024)S(1)} %reshape.1307), kind=kCustom, calls=%fused_computation | custom fusion | bytes 196608 | tf_op jit(solution)/shard_map/gather | solution.py:185
  1242.8 47.0 %all_to_all.15 = f32[128,1,320]{2,1,0:T(1,128)S(1)} all-to-all(f32[128,1,320]{2,1,0:T(1,128)S(1)} %reshape.1367), channel_id=1, replica_groups=mesh['grid'=2,'px'=16,'py'=8] {'px','py'}, dimensions={0} | all-to-all | bytes 327680 | tf_op jit(solution)/shard_map/all_to_all | solution.py:189
  1293.2 57.5 %collective-permute-start.5 = (f32[128,8,8,5]{0,2,3,1:T(8,128)S(1)}, f32[128,8,8,5]{0,2,3,1:T(8,128)S(1)}, u32[]{:S(2)}, u32[]{:S(2)}) collective-permute-start(f32[128,8,8,5]{0,2,3,1:T(8,128)S(1)} %copy.80), channel_id=1, source_target_pairs={{0,128},{128,0},{1,129},{129,1},{2,130},{130,2},{3,131},{131,3},{4... | collective-permute-start | bytes 491528 | tf_op jit(solution)/shard_map/ppermute | solution.py:16
  1362.1 51.3 %scatter_fusion = f32[64,5,1024]{1,2,0:T(8,128)} fusion(f32[64,5,1024]{1,2,0:T(8,128)} %bitcast.505, s32[512]{0:T(512)S(1)} %bitcast.508, f32[512,5]{1,0:T(8,128)S(1)} %multiply_reduce_fusion.16), kind=kCustom, calls=%fused_computation.4 | custom fusion | bytes 34816 | tf_op jit(solution)/shard_map/scatter | solution.py:195
  1413.4 20.4 %copy.84 = f32[1,8,8,5,1024]{4,2,3,1,0:T(8,128)} copy(f32[1,8,8,5,1024]{3,4,2,1,0:T(8,128)} %bitcast.506) | data formatting | bytes 2621440 | tf_op jit(solution)/shard_map/broadcast_in_dim;reshape | solution.py:198
  (4688 shorter events, 855.0 us)
Async XLA Ops:
  5.5 15.8 %collective-permute-start.4 = (s32[128,8,8]{2,1,0:T(8,128)S(1)}, s32[128,8,8]{2,1,0:T(8,128)S(1)}, u32[]{:S(2)}, u32[]{:S(2)}) collective-permute-start(s32[128,8,8]{2,1,0:T(8,128)S(1)} %bitcast.514), channel_id=1, source_target_pairs={{0,128},{128,0},{1,129},{129,1},{2,130},{130,2},{3,131},{131,3},{4... | collective-permute-start | bytes 98312 | tf_op jit(solution)/shard_map/ppermute | solution.py:16
  22.2 955.1 %all-to-all-start = ((s32[128,4,8]{2,1,0:T(4,128)}), s32[128,4,8]{2,1,0:T(4,128)S(1)}, u32[]{:S(2)}, u32[]{:S(2)}) async-start(s32[128,4,8]{2,1,0:T(4,128)} %get-tuple-element.801), calls=%async_computation | async-start | bytes 524288 | tf_op jit(solution)/shard_map/all_to_all | solution.py:32
  160.6 14.2 collective-permute-start.2
  175.8 14.2 collective-permute-start.2
  177.7 13.2 collective-permute-start.3
  198.7 16.3 %collective-permute-start.2 = (f32[8,5,128]{2,1,0:T(8,128)S(1)}, f32[8,5,128]{2,1,0:T(8,128)S(1)}, u32[]{:S(2)}, u32[]{:S(2)}) collective-permute-start(f32[8,5,128]{2,1,0:T(8,128)S(1)} %get-tuple-element.1261), channel_id=1, source_target_pairs={{0,1},{1,2},{2,3},{3,4},{4,5},{5,6},{6,7},{8,9},{9,10},{10,11},{11... | collective-permute-start | bytes 61448 | tf_op jit(solution)/shard_map/while/body/eval_jaxpr/ppermute | solution.py:12
  216.0 12.3 collective-permute-start.2
  217.9 11.3 collective-permute-start.3
  229.2 11.8 collective-permute-start.2
  231.2 10.9 collective-permute-start.3
  242.0 12.3 collective-permute-start.2
  244.4 10.9 collective-permute-start.3
  255.3 12.2 collective-permute-start.2
  257.2 11.2 collective-permute-start.3
  268.5 11.7 collective-permute-start.2
  281.2 12.3 collective-permute-start.2
  294.4 13.5 collective-permute-start.2
  296.4 12.6 collective-permute-start.3
  317.6 12.3 collective-permute-start.2
  421.3 11.6 collective-permute-start.1
  621.4 198.2 %collective-permute-start = (f32[8,5,128]{2,1,0:T(8,128)S(1)}, f32[8,5,128]{2,1,0:T(8,128)S(1)}, u32[]{:S(2)}, u32[]{:S(2)}) collective-permute-start(f32[8,5,128]{2,1,0:T(8,128)S(1)} %get-tuple-element.1297), channel_id=1, source_target_pairs={{1,0},{2,1},{3,2},{4,3},{5,4},{6,5},{7,6},{9,8},{10,9},{11,10},{12... | collective-permute-start | bytes 61448 | tf_op jit(solution)/shard_map/while/body/eval_jaxpr/ppermute | solution.py:12
  622.7 196.9 %collective-permute-start.1 = (f32[8,5,128]{2,1,0:T(8,128)S(1)}, f32[8,5,128]{2,1,0:T(8,128)S(1)}, u32[]{:S(2)}, u32[]{:S(2)}) collective-permute-start(f32[8,5,128]{2,1,0:T(8,128)S(1)} %get-tuple-element.1296), channel_id=1, source_target_pairs={{8,0},{16,8},{24,16},{32,24},{40,32},{48,40},{56,48},{64,56},{72,6... | collective-permute-start | bytes 61448 | tf_op jit(solution)/shard_map/while/body/eval_jaxpr/ppermute | solution.py:12
  977.3 18.9 %all-to-all-start.1 = ((s32[128,4,8]{2,1,0:T(4,128)}), s32[128,4,8]{2,1,0:T(4,128)S(1)}, u32[]{:S(2)}, u32[]{:S(2)}) async-start(s32[128,4,8]{2,1,0:T(4,128)} %get-tuple-element.802), calls=%async_computation.1 | async-start | bytes 524288 | tf_op jit(solution)/shard_map/all_to_all | solution.py:32
  1293.2 58.5 %collective-permute-start.5 = (f32[128,8,8,5]{0,2,3,1:T(8,128)S(1)}, f32[128,8,8,5]{0,2,3,1:T(8,128)S(1)}, u32[]{:S(2)}, u32[]{:S(2)}) collective-permute-start(f32[128,8,8,5]{0,2,3,1:T(8,128)S(1)} %copy.80), channel_id=1, source_target_pairs={{0,128},{128,0},{1,129},{129,1},{2,130},{130,2},{3,131},{131,3},{4... | collective-permute-start | bytes 491528 | tf_op jit(solution)/shard_map/ppermute | solution.py:16
  (103 other events, 876.9 us)
where the time goes:
time: 1440 us; the launch traced here: 1430 us
  local copies, waits for them, and re-layouts  440 us (31%)
  starting transfers between devices  440 us (31%)
  waiting for transfers between devices  425 us (30%)
  blocking collectives  47 us (3%)
  other arithmetic  46.8 us (3%)
  loops' own time  35 us (2%)
    ppermute x120, waiting for transfers between devices, from_behind(): return lax.ppermute(block, axis, route)  413 us
    ppermute x120, starting transfers between devices, from_behind(): return lax.ppermute(block, axis, route)  359 us
    gather x4, local copies, waits for them, and re-layouts, lookup(): flat_cells[index_list // pencil_length, :, index_list % pencil_length]  242 us
    ppermute x2, starting transfers between devices, swapped(): lax.ppermute(array, axis, [(i, i ^ 1 << distance) for i in range(lax.axis...  60.7 us
    scatter x1, local copies, waits for them, and re-layouts, local(): flat_cells.at[receptor_list // pencil_length, :, receptor_list % pencil_l...  51.3 us
    all_to_all x1, blocking collectives, local(): lax.all_to_all(values, ('px', 'py'), split_axis=0, concat_axis=0, tiled=T...  47 us

commit v1 on v0

v1 whole, which is shorter than its diff:
```python
import functools

import jax
import jax.numpy as jnp
from jax import lax
from jax.experimental import pallas as pl
from jax.experimental.pallas import tpu as pltpu
from jax.sharding import PartitionSpec as P

MESH = pl.DeviceIdType.MESH
LANES = 128
KB = 8
STEPS = 15
ROWS = 34
SLOTS_I = 22
STEP_ROWS = ROWS * 8
UP, LEFT, DOWN, RIGHT = range(4)


def sweep_kernel(nx, ny, inv_h, res_h, cou_h, out_h, data, star, swept, outs, fin, fout, load_sem, out_sem, send_sem, recv_sem):
    px, py = lax.axis_index("px"), lax.axis_index("py")
    depth = px + py
    deepest = nx + ny - 2
    has_source = {UP: px > 0, LEFT: py > 0, DOWN: px < nx - 1, RIGHT: py < ny - 1}
    has_target = {UP: px < nx - 1, LEFT: py < ny - 1, DOWN: px > 0, RIGHT: py > 0}
    target = {UP: {"px": px + 1}, LEFT: {"py": py + 1}, DOWN: {"px": px - 1}, RIGHT: {"py": py - 1}}

    def lanes(block):
        return pl.ds(pl.multiple_of(block * LANES, LANES), LANES)

    def load_block(block, carry):
        def load_row(row, inner):
            slot = 14 - row
            pltpu.make_async_copy(inv_h.at[row, :, :, lanes(block)], data.at[block, slot, pl.ds(0, 25)], load_sem.at[block]).start()
            pltpu.make_async_copy(res_h.at[row, :, :, lanes(block)], data.at[block, slot, pl.ds(25, 5)], load_sem.at[block]).start()
            pltpu.make_async_copy(cou_h.at[row, :, :, lanes(block)], data.at[block, slot, pl.ds(30, 4)], load_sem.at[block]).start()
            return inner

        return lax.fori_loop(0, 8, load_row, carry)

    lax.fori_loop(0, KB, load_block, 0)

    for kind in range(4):

        @pl.when(jnp.logical_not(has_source[kind]))
        def _(kind=kind):
            fin[kind] = jnp.zeros((KB, 5, 8, LANES), jnp.float32)

    barrier = pltpu.get_barrier_semaphore()
    for kind in range(4):

        @pl.when(has_target[kind])
        def _(kind=kind):
            pl.semaphore_signal(barrier, inc=1, device_id=target[kind], device_id_type=MESH)

    inner_x = jnp.logical_and(px > 0, px < nx - 1)
    inner_y = jnp.logical_and(py > 0, py < ny - 1)
    pl.semaphore_wait(barrier, jnp.where(inner_x, 2, 1) + jnp.where(inner_y, 2, 1))

    flat = data.reshape(KB * SLOTS_I * STEP_ROWS, LANES)
    sub = lax.broadcasted_iota(jnp.int32, (8, LANES), 0)

    def face_copy(kind, block):
        return pltpu.make_async_remote_copy(
            src_ref=fout.at[kind, block],
            dst_ref=fin.at[kind, block],
            send_sem=send_sem.at[kind, block],
            recv_sem=recv_sem.at[kind, block],
            device_id=target[kind],
            device_id_type=MESH,
        )

    def receive(kind, block):
        @pl.when(has_source[kind])
        def _():
            face_copy(kind, block).wait_recv()

    def send(kind, block, values, first, stride):
        for c in range(5):
            fout[kind, block, c] = values[pl.ds(block * (STEPS * 40) + c * 8 + first, 8, stride=stride), :]

        @pl.when(has_target[kind])
        def _():
            face_copy(kind, block).start()

    def entry(block, step, row):
        return flat[pl.ds(block * (SLOTS_I * STEP_ROWS) + (14 - step) * STEP_ROWS + row * 8, 8, stride=STEP_ROWS + 1), :]

    def product(block, step, vector):
        result = []
        for r in range(5):
            terms = [entry(block, step, r * 5 + c) * vector[c] for c in range(5)]
            result.append((terms[0] + terms[1]) + (terms[2] + terms[3]) + terms[4])
        return result

    def at_step(block, step, c):
        return pl.ds(pl.multiple_of(block * (STEPS * 40) + (step * 5 + c) * 8, 8), 8)

    def forward(block):
        pltpu.make_async_copy(data.at[block, pl.ds(7, 8)], data.at[block, pl.ds(7, 8)], load_sem.at[block]).wait()
        receive(UP, block)
        receive(LEFT, block)
        value = [jnp.zeros((8, LANES), jnp.float32)] * 5
        for step in range(STEPS):
            low_i, low_j = entry(block, step, 30), entry(block, step, 31)
            vector = []
            for c in range(5):
                upper = value[c]
                left = pltpu.roll(value[c], 1, 0)
                if step < 8:
                    upper = jnp.where(sub == step, fin[UP, block, c], upper)
                    face = jnp.broadcast_to(fin[LEFT, block, c, pl.ds(step, 1), :], (8, LANES))
                    left = jnp.where(sub == 0, face, left)
                vector.append(entry(block, step, 25 + c) + low_i * upper + low_j * left)
            value = product(block, step, vector)
            for c in range(5):
                star[at_step(block, step, c), :] = value[c]
        send(UP, block, star, 7 * 40, 41)
        send(LEFT, block, star, 7 * 40 + 7, 40)

    def backward(block):
        receive(DOWN, block)
        receive(RIGHT, block)
        value = [jnp.zeros((8, LANES), jnp.float32)] * 5
        for step in reversed(range(STEPS)):
            up_i, up_j = entry(block, step, 32), entry(block, step, 33)
            vector = []
            for c in range(5):
                lower = value[c]
                right = pltpu.roll(value[c], 7, 0)
                if step >= 7:
                    lower = jnp.where(sub == step - 7, fin[DOWN, block, c], lower)
                    face = jnp.broadcast_to(fin[RIGHT, block, c, pl.ds(step - 7, 1), :], (8, LANES))
                    right = jnp.where(sub == 7, face, right)
                vector.append(up_i * lower + up_j * right)
            added = product(block, step, vector)
            value = [star[at_step(block, step, c), :] + added[c] for c in range(5)]
            for c in range(5):
                swept[at_step(block, step, c), :] = value[c]
        send(DOWN, block, swept, 0, 41)
        send(RIGHT, block, swept, 0, 40)
        for row in range(8):
            for c in range(5):
                outs[block, row, c] = swept[pl.ds(block * (STEPS * 40) + (row * 5 + c) * 8, 8, stride=41), :]
        pltpu.make_async_copy(outs.at[block], out_h.at[:, :, :, lanes(block)], out_sem.at[block]).start()

    def turn(number, carry):
        corner = depth == deepest
        forth = jnp.where(corner, lax.rem(number, 2) == 0, number < KB)
        block = jnp.where(corner, number // 2, lax.rem(number, KB))

        @pl.when(forth)
        def _():
            forward(block)

        @pl.when(jnp.logical_not(forth))
        def _():
            backward(block)

        return carry

    lax.fori_loop(0, 2 * KB, turn, 0)

    def finish(block, carry):
        pltpu.make_async_copy(outs.at[block], out_h.at[:, :, :, lanes(block)], out_sem.at[block]).wait()
        for kind in range(4):

            @pl.when(has_target[kind])
            def _(kind=kind):
                face_copy(kind, block).wait_send()

        return carry

    lax.fori_loop(0, KB, finish, 0)


def sweep(nx, ny, inverses, residual, couplings):
    any_space = pl.BlockSpec(memory_space=pl.ANY)
    return pl.pallas_call(
        functools.partial(sweep_kernel, nx, ny),
        out_shape=jax.ShapeDtypeStruct((8, 5, 8, KB * LANES), jnp.float32),
        in_specs=[any_space] * 3,
        out_specs=any_space,
        scratch_shapes=[
            pltpu.VMEM((KB, SLOTS_I, ROWS, 8, LANES), jnp.float32),
            pltpu.VMEM((KB * STEPS * 40, LANES), jnp.float32),
            pltpu.VMEM((KB * STEPS * 40, LANES), jnp.float32),
            pltpu.VMEM((KB, 8, 5, 8, LANES), jnp.float32),
            pltpu.VMEM((4, KB, 5, 8, LANES), jnp.float32),
            pltpu.VMEM((4, KB, 5, 8, LANES), jnp.float32),
            pltpu.SemaphoreType.DMA((KB,)),
            pltpu.SemaphoreType.DMA((KB,)),
            pltpu.SemaphoreType.DMA((4, KB)),
            pltpu.SemaphoreType.DMA((4, KB)),
        ],
        compiler_params=pltpu.CompilerParams(collective_id=0, has_side_effects=True, vmem_limit_bytes=48 << 20),
        name="sweep",
    )(inverses, residual, couplings)


def load_field(swept_h, field, sem):
    for block in range(KB):
        pltpu.make_async_copy(swept_h.at[:, :, :, pl.ds(block * LANES, LANES)], field.at[block], sem.at[block]).start()
    for block in range(KB):
        pltpu.make_async_copy(swept_h.at[:, :, :, pl.ds(block * LANES, LANES)], field.at[block], sem.at[block]).wait()


def cell_rows(start):
    return pl.ds(start, 5, stride=8)


def interpolate_kernel(slots, count, start_ref, table_ref, swept_h, out_ref, field, mask, sem):
    lane = lax.broadcasted_iota(jnp.int32, (8, LANES), 1)

    def build(group, carry):
        rows = pl.ds(pl.multiple_of(group * 8, 8), 8)
        block = table_ref[rows, :]
        for d in range(count):
            place = jnp.broadcast_to(block[:, d : d + 1], (8, LANES)).astype(jnp.int32)
            weight = jnp.broadcast_to(block[:, count + d : count + d + 1], (8, LANES))
            mask[d, rows, :] = jnp.where(lane == place, weight, 0.0)
        return carry

    lax.fori_loop(0, slots // 8, build, 0)
    load_field(swept_h, field, sem)
    flat = field.reshape(KB * 8 * 5 * 8, LANES)
    lane5 = lax.broadcasted_iota(jnp.int32, (5, LANES), 1)

    def gather(group, carry):
        result = jnp.zeros((5, LANES), jnp.float32)
        for unit in range(16):
            slot = group * 16 + unit
            terms = []
            for d in range(count):
                start = start_ref[slot * count + d]
                cells = flat[cell_rows(start), :]
                terms.append(cells * mask[d, pl.ds(slot, 1), :])
            while len(terms) > 1:
                terms = [terms[i] + terms[i + 1] for i in range(0, len(terms), 2)]
            total = jnp.sum(terms[0], axis=1, keepdims=True)
            result = jnp.where(lane5 == unit, total, result)
        out_ref[group] = result
        return carry

    lax.fori_loop(0, slots // 16, gather, 0)


def interpolate(start, table, swept):
    slots = table.shape[0]
    count = start.shape[0] // slots
    return pl.pallas_call(
        functools.partial(interpolate_kernel, slots, count),
        out_shape=jax.ShapeDtypeStruct((slots // 16, 5, LANES), jnp.float32),
        in_specs=[
            pl.BlockSpec(memory_space=pltpu.SMEM),
            pl.BlockSpec(memory_space=pltpu.VMEM),
            pl.BlockSpec(memory_space=pl.ANY),
        ],
        out_specs=pl.BlockSpec(memory_space=pltpu.VMEM),
        scratch_shapes=[
            pltpu.VMEM((KB, 8, 5, 8, LANES), jnp.float32),
            pltpu.VMEM((count, slots, LANES), jnp.float32),
            pltpu.SemaphoreType.DMA((KB,)),
        ],
        compiler_params=pltpu.CompilerParams(vmem_limit_bytes=24 << 20),
        name="interpolate",
    )(start, table, swept)


def refresh_kernel(receptors, start_ref, shift_ref, lane_ref, group_ref, value_ref, swept_h, out_h, field, sem, out_sem):
    load_field(swept_h, field, sem)
    flat = field.reshape(KB * 8 * 5 * 8, LANES)
    lane = lax.broadcasted_iota(jnp.int32, (8, LANES), 1)

    def place(batch, carry):
        for unit in range(8):
            r = batch * 8 + unit
            rows = cell_rows(start_ref[r])
            moved = pltpu.roll(value_ref[group_ref[r]], shift_ref[r], 1)
            old = flat[rows, :]
            flat[rows, :] = jnp.where(lane[:5] == lane_ref[r], moved[:5], old)
        return carry

    lax.fori_loop(0, receptors // 8, place, 0)
    for block in range(KB):
        pltpu.make_async_copy(field.at[block], out_h.at[:, :, :, pl.ds(block * LANES, LANES)], out_sem.at[block]).start()
    for block in range(KB):
        pltpu.make_async_copy(field.at[block], out_h.at[:, :, :, pl.ds(block * LANES, LANES)], out_sem.at[block]).wait()


def refresh(start, shift, lane, group, values, swept):
    smem = pl.BlockSpec(memory_space=pltpu.SMEM)
    return pl.pallas_call(
        functools.partial(refresh_kernel, start.shape[0]),
        out_shape=jax.ShapeDtypeStruct(swept.shape, jnp.float32),
        in_specs=[smem] * 4 + [pl.BlockSpec(memory_space=pltpu.VMEM), pl.BlockSpec(memory_space=pl.ANY)],
        out_specs=pl.BlockSpec(memory_space=pl.ANY),
        scratch_shapes=[
            pltpu.VMEM((KB, 8, 5, 8, LANES), jnp.float32),
            pltpu.SemaphoreType.DMA((KB,)),
            pltpu.SemaphoreType.DMA((KB,)),
        ],
        compiler_params=pltpu.CompilerParams(vmem_limit_bytes=16 << 20),
        name="refresh",
    )(start, shift, lane, group, values, swept)


def swapped(array, axis, distance):
    return lax.ppermute(array, axis, [(i, i ^ 1 << distance) for i in range(lax.axis_size(axis))])


def cell_start(cell):
    pencil, k = cell // 1024, cell % 1024
    return (k // LANES * 8 + pencil // 8) * 40 + pencil % 8


def local(residual, inverses, couplings, receptors, owners, donors, weights):
    nx, ny = lax.axis_size("px"), lax.axis_size("py")
    by_row = lambda a: jnp.transpose(a[0], (0, 2, 1, 3))
    receptor_list = receptors[0, 0, 0]
    owner_list = owners[0, 0, 0, :, 0]
    donor_list = donors[0, 0, 0]
    weight_list = weights[0, 0, 0]
    receptor_count, count = donor_list.shape
    owner_count = nx * ny
    slot_count = max(2, 2 * receptor_count // owner_count)
    slots = owner_count * slot_count
    onehot = (owner_list[:, None] == jnp.arange(owner_count, dtype=jnp.int32)[None, :]).astype(jnp.int32)
    slot_rank = jnp.sum((jnp.cumsum(onehot, axis=0) - 1) * onehot, axis=1)
    slot_place = owner_list * slot_count + slot_rank
    asked = jnp.concatenate([donor_list.astype(jnp.float32), weight_list], axis=1)
    request = jnp.zeros((slots, 2 * count), jnp.float32).at[slot_place].set(asked)
    request = swapped(request.reshape(owner_count, slot_count * 2 * count), "grid", 0)
    request = lax.all_to_all(request, ("px", "py"), split_axis=0, concat_axis=0, tiled=True)
    request = request.reshape(slots, 2 * count)
    cell = request[:, :count].astype(jnp.int32)
    table = jnp.concatenate([(cell % LANES).astype(jnp.float32), request[:, count:]], axis=1)
    table = jnp.pad(table, ((0, 0), (0, LANES - 2 * count)))

    swept = sweep(nx, ny, by_row(inverses), by_row(residual), by_row(couplings))

    answer = interpolate(cell_start(cell).reshape(slots * count), table, swept)
    answer = jnp.transpose(answer[:, :, :16], (0, 2, 1)).reshape(owner_count, slot_count * 5)
    answer = lax.all_to_all(answer, ("px", "py"), split_axis=0, concat_axis=0, tiled=True)
    answer = swapped(answer, "grid", 0)
    groups = slots // LANES
    values = jnp.transpose(answer.reshape(groups, LANES, 5), (0, 2, 1))
    values = jnp.pad(values, ((0, 0), (0, 3), (0, 0)))
    lane = receptor_list % LANES
    shift = (lane - slot_place) % LANES
    update = refresh(cell_start(receptor_list), shift, lane, slot_place // LANES, values, swept)
    return jnp.transpose(update, (0, 2, 1, 3))[None]


def solution(mesh):
    placed = (
        P("grid", "px", "py", None, None),
        P("grid", "px", "py", None, None),
        P("grid", "px", "py", None, None),
        P("grid", "px", "py", None),
        P("grid", "px", "py", None, None),
        P("grid", "px", "py", None, None),
        P("grid", "px", "py", None, None),
    )
    return jax.shard_map(
        local,
        mesh=mesh,
        in_specs=placed,
        out_specs=P("grid", "px", "py", None, None),
        check_vma=False,
    )
```

time: 1440 us -> 228 us (0.16)
  local copies, waits for them, and re-layouts: 440 us -> 7.06 us
  waiting for transfers between devices: 425 us -> 1.91 us
  starting transfers between devices: 440 us -> 57 us
  Pallas kernels: 0 us -> 143 us
  other arithmetic: 46.8 us -> 3 us
  loops' own time: 35 us -> 0 us
  blocking collectives: 47 us -> 16.1 us
    ppermute x120 -> x0, waiting for transfers between devices: 413 us -> none  [from_behind(): return lax.ppermute(block, axis, route)]
    ppermute x120 -> x0, starting transfers between devices: 359 us -> none  [from_behind(): return lax.ppermute(block, axis, route)]
    gather x5 -> x0, local copies, waits for them, and re-layouts: 245 us -> none  [the longest x4 242 us: lookup(): flat_cells[index_list // pencil_length, :, index_list % pencil_length]]
    pallas_call x0 -> x3, Pallas kernels: none -> 143 us  [the longest x1 107 us: sweep(): pl.pallas_call(functools.partial(sweep_kernel, nx, ny), out_shape=jax.Sha...]
    dynamic_slice x48 -> x0, local copies, waits for them, and re-layouts: 51.6 us -> none  [the longest x16 21.3 us: slices(): lax.dynamic_slice_in_dim(inverse_local, offset, block_width, 3)]
    scatter x2 -> x1, local copies, waits for them, and re-layouts: 53.1 us -> 1.84 us  [local(): jnp.zeros((slots, 2 * count), jnp.float32).at[slot_place].set(asked)]
    another operation x78 -> x0, loops' own time: 35 us -> none  [the longest x8 17.3 us: sweep_backward(): lax.scan(row_step, from_rows, (star_part, inverse_part, coupling_part, fr...]
    all_to_all x1, blocking collectives: 47 us -> 16.1 us  [local(): lax.all_to_all(answer, ('px', 'py'), split_axis=0, concat_axis=0, tiled=T...]
where the time goes in v1:
time: 228 us
  Pallas kernels  143 us (63%)
  starting transfers between devices  57 us (25%)
  blocking collectives  16.1 us (7%)
  local copies, waits for them, and re-layouts  7.06 us (3%)
  other arithmetic  3 us (1%)
    pallas_call x1, Pallas kernels, sweep(): pl.pallas_call(functools.partial(sweep_kernel, nx, ny), out_shape=jax.Sha...  107 us
    ppermute x2, starting transfers between devices, swapped(): lax.ppermute(array, axis, [(i, i ^ 1 << distance) for i in range(lax.axis...  43.2 us
    pallas_call x1, Pallas kernels, interpolate(): pl.pallas_call(functools.partial(interpolate_kernel, slots, count), out_s...  27.6 us
    all_to_all x1, blocking collectives, local(): lax.all_to_all(answer, ('px', 'py'), split_axis=0, concat_axis=0, tiled=T...  16.1 us
    all_to_all x1, starting transfers between devices, local(): lax.all_to_all(request, ('px', 'py'), split_axis=0, concat_axis=0, tiled=...  13.8 us
    pallas_call x1, Pallas kernels, refresh(): pl.pallas_call(functools.partial(refresh_kernel, start.shape[0]), out_sha...  8.21 us
  transfers between devices with their start and end apart: 3, of which 2 were waited for; matrix products, arithmetic and copies ran while one was open for 1% of the time, Pallas kernels for 47%

profile of v1, /device:TPU:1, one launch (start us, length us, event | category | flops | bytes accessed | tf_op | source)
XLA Modules:
  0.0 227.8 jit_solution(2490860669503412121)
XLA Ops:
  0.0 0.9 copy.27
  0.9 0.2 fusion.16
  1.2 0.2 fusion.13
  1.6 1.8 scatter_custom_fusion
  3.5 0.2 reshape.68
  3.7 3.3 %collective-permute-start = (f32[128,128]{1,0:T(8,128)S(1)}, f32[128,128]{1,0:T(8,128)}, u32[]{:S(2)}, u32[]{:S(2)}) collective-permute-start(f32[128,128]{1,0:T(8,128)S(1)} %reshape.68), channel_id=1, source_target_pairs={{0,128},{128,0},{1,129},{129,1},{2,130},{130,2},{3,131},{131,3},{4... | collective-permute-start | bytes 196616 | tf_op jit(solution)/shard_map/ppermute | solution.py:309
  7.0 1.0 collective-permute-done
  8.0 13.8 %all-to-all-start = ((f32[128,1,128]{2,1,0:T(1,128)}), f32[128,1,128]{2,1,0:T(1,128)S(1)}, u32[]{:S(2)}, u32[]{:S(2)}) async-start(f32[128,1,128]{2,1,0:T(1,128)} %bitcast.12), calls=%async_computation | async-start | bytes 131072 | tf_op jit(solution)/shard_map/all_to_all | solution.py:334
  21.8 1.8 copy.36
  23.7 106.7 %sweep.1.swept_h = f32[8,5,8,1024]{3,2,1,0:T(8,128)S(1)} custom-call(f32[8,25,8,1024]{3,2,1,0:T(8,128)} %bitcast.44, f32[8,5,8,1024]{3,2,1,0:T(8,128)S(1)} %bitcast.43, f32[8,4,8,1024]{3,2,1,0:T(8,128)S(1)} %bitcast.42), custom_call_target="tpu_custom_call" | custom-call | tf_op jit(solution)/shard_map/sweep/pallas_call | solution.py:179
  130.4 0.5 broadcast.158
  130.9 0.8 reduce.3
  131.9 1.4 fusion.5
  133.3 0.2 slice.22
  133.5 0.2 reshape.70.start_ref
  133.8 0.2 select_maximum_fusion.table_ref
  134.0 27.6 %interpolate.1 = f32[64,5,128]{2,1,0:T(8,128)S(1)} custom-call(s32[8192]{0:T(1024)S(1)} %reshape.70.start_ref, f32[1024,128]{1,0:T(8,128)S(1)} %select_maximum_fusion.table_ref, f32[8,5,8,1024]{3,2,1,0:T(8,128)S(1)} %sweep.1.swept_h), custom_call_target="tpu_custom_call" | custom-call | tf_op jit(solution)/shard_map/interpolate/pallas_call | solution.py:251
  161.6 0.4 copy.32
  162.1 0.2 all_to_all.16
  162.3 16.1 %all_to_all.21 = f32[128,1,40]{2,1,0:T(1,128)S(1)} all-to-all(f32[128,1,40]{2,1,0:T(1,128)S(1)} %bitcast.45), channel_id=1, replica_groups=mesh['grid'=2,'px'=16,'py'=8] {'px','py'}, dimensions={0} | all-to-all | bytes 40960 | tf_op jit(solution)/shard_map/all_to_all | solution.py:344
  178.4 39.9 %collective-permute-start.1 = (f32[128,40]{1,0:T(8,128)S(1)}, f32[128,40]{1,0:T(8,128)S(1)}, u32[]{:S(2)}, u32[]{:S(2)}) collective-permute-start(f32[128,40]{1,0:T(8,128)S(1)} %bitcast.47), channel_id=1, source_target_pairs={{0,128},{128,0},{1,129},{129,1},{2,130},{130,2},{3,131},{131,3},{4... | collective-permute-start | bytes 61448 | tf_op jit(solution)/shard_map/ppermute | solution.py:309
  218.3 0.9 collective-permute-done.1
  219.4 0.2 copy.34
  219.5 8.2 %refresh.1 = f32[8,5,8,1024]{3,2,1,0:T(8,128)} custom-call(s32[512]{0:T(512)S(1)} %get-tuple-element.10.start_ref, s32[512]{0:T(512)S(1)} %get-tuple-element.8.shift_ref, s32[512]{0:T(512)S(1)} %get-tuple-element.9.lane_ref, s32[512]{0:T(512)S(1)} %get-tuple-element.7.group_ref, f32[8,8,128]{2,1,0:T(8,128)S(1)} %pad.9.value_ref, ...), custom_call_target="tpu_custom_call" | custom-call | tf_op jit(solution)/shard_map/refresh/pallas_call | solution.py:293
  (25 shorter events, 0.7 us)
Async XLA Ops:
  0.0 1.2 copy-start.1
  0.0 1.5 copy-start.2
  0.0 1.5 copy-start.3
  3.5 20.2 %copy-start = (f32[1,8,8,5,1024]{4,2,3,1,0:T(8,128)S(1)}, f32[1,8,8,5,1024]{4,2,3,1,0:T(8,128)}, u32[]{:S(2)}) copy-start(f32[1,8,8,5,1024]{4,2,3,1,0:T(8,128)} %param.7) | copy-start | bytes 3932164
  3.7 4.3 %collective-permute-start = (f32[128,128]{1,0:T(8,128)S(1)}, f32[128,128]{1,0:T(8,128)}, u32[]{:S(2)}, u32[]{:S(2)}) collective-permute-start(f32[128,128]{1,0:T(8,128)S(1)} %reshape.68), channel_id=1, source_target_pairs={{0,128},{128,0},{1,129},{129,1},{2,130},{130,2},{3,131},{131,3},{4... | collective-permute-start | bytes 196616 | tf_op jit(solution)/shard_map/ppermute | solution.py:309
  8.0 122.3 %all-to-all-start = ((f32[128,1,128]{2,1,0:T(1,128)}), f32[128,1,128]{2,1,0:T(1,128)S(1)}, u32[]{:S(2)}, u32[]{:S(2)}) async-start(f32[128,1,128]{2,1,0:T(1,128)} %bitcast.12), calls=%async_computation | async-start | bytes 131072 | tf_op jit(solution)/shard_map/all_to_all | solution.py:334
  161.6 56.7 %copy-start.4 = (s32[1,1,1,512]{3,2,1,0:T(1,128)S(1)}, s32[1,1,1,512]{3,2,1,0:T(1,128)}, u32[]{:S(2)}) copy-start(s32[1,1,1,512]{3,2,1,0:T(1,128)} %param.10) | copy-start | bytes 6148
  178.4 40.8 %collective-permute-start.1 = (f32[128,40]{1,0:T(8,128)S(1)}, f32[128,40]{1,0:T(8,128)S(1)}, u32[]{:S(2)}, u32[]{:S(2)}) collective-permute-start(f32[128,40]{1,0:T(8,128)S(1)} %bitcast.47), channel_id=1, source_target_pairs={{0,128},{128,0},{1,129},{129,1},{2,130},{130,2},{3,131},{131,3},{4... | collective-permute-start | bytes 61448 | tf_op jit(solution)/shard_map/ppermute | solution.py:309
